TPU v7x, 32 devices: a whole 2x2x4 slice. The times are simulated.
32 devices in a mesh: layer: 2 (over x), row: 4 (over z), col: 4 (over y, core).
Axes of the slice: x: 2, y: 2, z: 4, core: 2. Of those that a mesh axis runs over, the one named last changes fastest.
Arguments:
- left_matrix: float32 [2, 1024, 16384], P(None, 'row', 'col'), may hold values from -6 to 6
- right_matrix: float32 [2, 16384, 512], P(None, 'row', 'col'), may hold values from -0.03125 to 0.03125
Outputs:
- product: float32 [2, 1024, 512], P(None, 'row', 'col')
All inputs are finite; a program needn't handle non-finite values.
Results may differ from a plain program's by a relative error of at most 0.000071.
Values sent between devices are 32-bit elements; how exact they have to be, the bound alone decides.
A program may use at most 128 MiB of HBM per device.

v0:
```python
import jax
import jax.numpy as jnp
from jax import lax
from jax.sharding import PartitionSpec as P


def gauss_fold(right_whole, site_rows, cols_out):
    right_real = right_whole[0]
    right_imag = right_whole[1]
    right_total = right_real + right_imag
    highest = lax.Precision.HIGHEST
    empty = jnp.zeros((site_rows, cols_out), jnp.float32)

    def accumulate(totals, segment, offset):
        left_real = segment[0]
        left_imag = segment[1]
        first_term = jnp.dot(
            left_real, right_real, precision=highest, preferred_element_type=jnp.float32
        )
        second_term = jnp.dot(
            left_imag, right_imag, precision=highest, preferred_element_type=jnp.float32
        )
        third_term = jnp.dot(
            left_real + left_imag,
            right_total,
            precision=highest,
            preferred_element_type=jnp.float32,
        )
        return (first_term, second_term, third_term)

    return (accumulate, (empty, empty, empty))


def combine_terms(totals):
    first_term, second_term, third_term = totals
    return jnp.stack([first_term - second_term, third_term - first_term - second_term])


def local(left_matrix, right_matrix):
    layers = lax.axis_size("layer")
    layer_index = lax.axis_index("layer")
    local_rows = left_matrix.shape[1]
    local_cols = right_matrix.shape[2]
    left_width = left_matrix.shape[2]
    right_height = right_matrix.shape[1]
    share_width = left_width // layers
    group_count = right_height // left_width
    left_own = lax.dynamic_slice_in_dim(left_matrix, layer_index * share_width, share_width, 2)
    right_view = right_matrix.reshape(2, group_count, layers, share_width, local_cols)
    right_own = lax.dynamic_slice_in_dim(right_view, layer_index, 1, 2)
    right_own = right_own.reshape(2, group_count * share_width, local_cols)
    right_whole = lax.all_gather(right_own, "row", axis=1, tiled=True)
    accumulate, initial = gauss_fold(right_whole, local_rows, local_cols)
    totals = accumulate(initial, lax.all_gather(left_own, "col", axis=2, tiled=True), jnp.int32(0))
    partial_product = combine_terms(totals)
    product = lax.psum(partial_product, "layer")
    return product


def solution(mesh):
    in_specs = (P(None, "row", "col"), P(None, "row", "col"))
    out_specs = P(None, "row", "col")
    return jax.shard_map(local, mesh=mesh, in_specs=in_specs, out_specs=out_specs, check_vma=False)
```

profile of v0, /device:TPU:0, one launch (start us, length us, event | category | flops | bytes accessed | tf_op | source)
XLA Modules:
  0.0 329.2 jit_solution(11281705026312441378)
XLA Ops:
  6.5 0.0 all-gather.6.cloned.1.call-start
  6.5 3.1 constant_dynamic-slice_fusion
  9.6 0.0 all-gather.6.cloned.1.call-update
  9.6 0.0 all-gather.4.cloned.1.call-start
  9.7 4.7 %constant_dynamic-slice_fusion.1 = f32[2,256,2048]{2,1,0:T(8,128)} fusion(f32[2,256,4096]{2,1,0:T(8,128)} %param.2, s32[]{:T(128)S(6)} %select_n.6), kind=kLoop, calls=%fused_computation.25 | loop fusion | bytes 8388612 | tf_op jit(solution)/shard_map/dynamic_slice | solution.py:48
  14.3 0.0 all-gather.4.cloned.1.call-update
  14.3 0.0 all-reduce.2.cloned.1.call-start
  14.4 147.7 %all-gather.6.cloned.1.call-done = f32[2,1,1,8192,128]{4,3,2,0,1:T(8,128)} async-done(((f32[2,1,1,2048,128]{4,3,2,0,1:T(8,128)}), f32[2,1,1,8192,128]{4,3,2,0,1:T(8,128)}) %all-gather.6.cloned.1.call-update) | async-done | bytes 8388624 | tf_op jit(solution)/shard_map/all_gather | solution.py:52
  162.1 105.7 %all-gather.4.cloned.1.call-done = f32[2,256,8192]{2,1,0:T(8,128)} async-done(((f32[2,256,2048]{2,1,0:T(8,128)}), f32[2,256,8192]{2,1,0:T(8,128)}) %all-gather.4.cloned.1.call-update) | async-done | bytes 16777232 | tf_op jit(solution)/shard_map/all_gather | solution.py:54
  267.8 0.0 copy-start
  267.8 9.9 %fusion.4 = f32[256,128]{1,0:T(8,128)S(1)} fusion(f32[2,256,8192]{2,1,0:T(8,128)} %all-gather.4.cloned.1.call-done, f32[2,1,1,8192,128]{4,3,2,0,1:T(8,128)} %all-gather.6.cloned.1.call-done), kind=kOutput, calls=%fused_computation.4 | convolution fusion | flops 3221225472 | bytes 12713984 | tf_op jit(solution)/shard_map/dot_general | solution.py:17
  277.7 9.8 %fusion.2 = f32[256,128]{1,0:T(8,128)S(1)} fusion(f32[2,256,8192]{2,1,0:T(8,128)} %all-gather.4.cloned.1.call-done, f32[2,1,1,8192,128]{4,3,2,0,1:T(8,128)} %all-gather.6.cloned.1.call-done), kind=kOutput, calls=%fused_computation.2 | convolution fusion | flops 3221225472 | bytes 12713984 | tf_op jit(solution)/shard_map/dot_general | solution.py:20
  287.6 0.0 copy-done
  287.6 9.2 %fusion.29 = f32[1,256,128]{2,1,0:T(8,128)S(1)} fusion(f32[256,128]{1,0:T(8,128)S(1)} %fusion.2, f32[256,128]{1,0:T(8,128)S(1)} %fusion.4, f32[2,1,1,8192,128]{4,3,2,0,1:T(8,128)} %all-gather.6.cloned.1.call-done, f32[2,256,8192]{2,1,0:T(8,128)S(1)} %copy-done), kind=kOutput, calls=%fused_computation.21 | convolution fusion | flops 3224436736 | bytes 25559040 | tf_op jit(solution)/shard_map/dot_general | solution.py:23
  296.8 0.7 pad_maximum_fusion
  297.5 0.0 all-reduce.2.cloned.1.call-update
  297.5 23.4 %all-reduce.2.cloned.1.call-done = f32[2,256,128]{2,1,0:T(8,128)} async-done(((f32[2,256,128]{2,1,0:T(8,128)}), f32[2,256,128]{2,1,0:T(8,128)}) %all-reduce.2.cloned.1.call-update) | async-done | bytes 262160 | tf_op jit(solution)/shard_map/psum | solution.py:56
  321.0 1.7 copy.4
  (1 shorter events, 0.0 us)
Async XLA Ops:
  6.5 155.6 %all-gather.6.cloned.1.call-start = ((), (), s32[]{:S(2)}) async-start(), calls=%async_computation.2 | async-start | bytes 10485760 | tf_op jit(solution)/shard_map/all_gather | solution.py:52
  9.6 258.2 %all-gather.4.cloned.1.call-start = ((), (), s32[]{:S(2)}) async-start(), calls=%async_computation | async-start | bytes 20971520 | tf_op jit(solution)/shard_map/all_gather | solution.py:54
  14.3 306.6 %all-reduce.2.cloned.1.call-start = ((), (), s32[]{:S(2)}) async-start(), calls=%async_computation.1 | async-start | bytes 524288 | tf_op jit(solution)/shard_map/psum | solution.py:56
  267.8 19.8 %copy-start = (f32[2,256,8192]{2,1,0:T(8,128)S(1)}, f32[2,256,8192]{2,1,0:T(8,128)}, u32[]{:S(2)}) copy-start(f32[2,256,8192]{2,1,0:T(8,128)} %all-gather.4.cloned.1.call-done) | copy-start | bytes 50331652
Sparse Core Ops, SparseCore 0:
  9.7 152.3 all-gather.5
  163.7 104.0 all-gather.3
  297.7 23.2 all-reduce.1
where the time goes:
time: 329 us
  waiting for transfers between devices  277 us (84%)
  matrix products  28.9 us (9%)
  between operations  13.2 us (4%)
  local copies, waits for them, and re-layouts  9.38 us (3%)
    all_gather x1, waiting for transfers between devices, local(): right_whole = lax.all_gather(right_own, 'row', axis=1, tiled=True)  148 us
    all_gather x1, waiting for transfers between devices, local(): lax.all_gather(left_own, 'col', axis=2, tiled=True)  106 us
    psum x1, waiting for transfers between devices, local(): product = lax.psum(partial_product, 'layer')  23.4 us
    dot_general x1, matrix products, accumulate(): jnp.dot(left_real, right_real, precision=highest, preferred_element_type=...  9.94 us
    dot_general x1, matrix products, accumulate(): jnp.dot(left_imag, right_imag, precision=highest, preferred_element_type=...  9.81 us
    dot_general x1, matrix products, accumulate(): jnp.dot(left_real + left_imag, right_total, precision=highest, preferred_...  9.2 us
  transfers between devices with their start and end apart: 3, of which 3 were waited for; matrix products, arithmetic and copies ran while one was open for 1% of the time, Pallas kernels for 0%

commit v1 on v0

--- a/solution.py
+++ b/solution.py
@@ -49,7 +49,12 @@
     right_view = right_matrix.reshape(2, group_count, layers, share_width, local_cols)
     right_own = lax.dynamic_slice_in_dim(right_view, layer_index, 1, 2)
     right_own = right_own.reshape(2, group_count * share_width, local_cols)
-    right_whole = lax.all_gather(right_own, "row", axis=1, tiled=True)
+    ring = [right_own]
+    for hop in range(3):
+        ring.append(lax.ppermute(ring[-1], "row", [(dev, (dev + 1) % 4) for dev in range(4)]))
+    right_whole = jnp.roll(
+        jnp.concatenate(ring[::-1], axis=1), (lax.axis_index("row") + 1) * ring[0].shape[1], axis=1
+    )
     accumulate, initial = gauss_fold(right_whole, local_rows, local_cols)
     totals = accumulate(initial, lax.all_gather(left_own, "col", axis=2, tiled=True), jnp.int32(0))
     partial_product = combine_terms(totals)

time: 329 us -> 240 us (0.73)
  waiting for transfers between devices: 277 us -> 166 us
  local copies, waits for them, and re-layouts: 9.38 us -> 27.8 us
    all_gather x1 -> x0, waiting for transfers between devices: 148 us -> none  [local(): right_whole = lax.all_gather(right_own, 'row', axis=1, tiled=True)]
    ppermute x0 -> x3, waiting for transfers between devices: none -> 144 us  [local(): lax.ppermute(ring[-1], 'row', [(dev, (dev + 1) % 4) for dev in range(4)])]
    all_gather x1, waiting for transfers between devices: 106 us -> 0.01 us  [local(): lax.all_gather(left_own, 'col', axis=2, tiled=True)]
    unnamed x3 -> x12, local copies, waits for them, and re-layouts: 1.67 us -> 19.8 us
  transfers between devices with their start and end apart: 3 -> 5, of which waited for: 3 -> 4; matrix products, arithmetic and copies ran while one was open for 1% -> 9% of each run, Pallas kernels for 0% -> 0%
where the time goes in v1:
time: 240 us
  waiting for transfers between devices  166 us (69%)
  matrix products  29.3 us (12%)
  local copies, waits for them, and re-layouts  27.8 us (12%)
  between operations  13.5 us (6%)
  starting transfers between devices  3.15 us (1%)
    ppermute x3, waiting for transfers between devices, local(): lax.ppermute(ring[-1], 'row', [(dev, (dev + 1) % 4) for dev in range(4)])  144 us
    psum x1, waiting for transfers between devices, local(): product = lax.psum(partial_product, 'layer')  21.2 us
    unnamed x12, local copies, waits for them, and re-layouts  19.8 us
    dot_general x1, matrix products, accumulate(): jnp.dot(left_real, right_real, precision=highest, preferred_element_type=...  9.94 us
    dot_general x1, matrix products, accumulate(): jnp.dot(left_imag, right_imag, precision=highest, preferred_element_type=...  9.82 us
    dot_general x1, matrix products, accumulate(): jnp.dot(left_real + left_imag, right_total, precision=highest, preferred_...  9.55 us
  transfers between devices with their start and end apart: 5, of which 4 were waited for; matrix products, arithmetic and copies ran while one was open for 9% of the time, Pallas kernels for 0%

profile of v1, /device:TPU:0, one launch (start us, length us, event | category | flops | bytes accessed | tf_op | source)
XLA Modules:
  0.0 240.1 jit_solution(14352232666211421458)
XLA Ops:
  6.5 0.0 all-gather.2.cloned.1.call-start
  6.5 4.8 %constant_dynamic-slice_fusion = f32[2,256,2048]{2,1,0:T(8,128)} fusion(f32[2,256,4096]{2,1,0:T(8,128)} %param.2, s32[]{:T(128)S(6)} %select_n.19), kind=kLoop, calls=%fused_computation.36 | loop fusion | bytes 8388612 | tf_op jit(solution)/shard_map/dynamic_slice | solution.py:48
  11.3 0.0 all-gather.2.cloned.1.call-update
  11.3 0.0 all-reduce.2.cloned.1.call-start
  11.4 1.7 dynamic-slice_bitcast_fusion
  13.1 3.1 %collective-permute-start = (f32[2,2048,128]{2,1,0:T(8,128)S(1)}, f32[2,2048,128]{2,1,0:T(8,128)S(1)}, u32[]{:S(2)}, u32[]{:S(2)}) collective-permute-start(f32[2,2048,128]{2,1,0:T(8,128)S(1)} %dynamic-slice_bitcast_fusion), channel_id=1, source_target_pairs={{0,4},{4,8},{8,12},{12,0},{1,5},{5,9},{9,13},{13,1},{2,6},{6,10},{... | collective-permute-start | bytes 6291464 | tf_op jit(solution)/shard_map/ppermute | solution.py:54
  16.2 47.7 %collective-permute-done = f32[2,2048,128]{2,1,0:T(8,128)S(1)} collective-permute-done((f32[2,2048,128]{2,1,0:T(8,128)S(1)}, f32[2,2048,128]{2,1,0:T(8,128)S(1)}, u32[]{:S(2)}, u32[]{:S(2)}) %collective-permute-start) | collective-permute-done | bytes 2097184 | tf_op jit(solution)/shard_map/ppermute | solution.py:54
  63.9 0.0 collective-permute-start.1
  63.9 48.7 %collective-permute-done.1 = f32[2,2048,128]{2,1,0:T(8,128)} collective-permute-done((f32[2,2048,128]{2,1,0:T(8,128)S(1)}, f32[2,2048,128]{2,1,0:T(8,128)}, u32[]{:S(2)}, u32[]{:S(2)}) %collective-permute-start.1) | collective-permute-done | bytes 2097184 | tf_op jit(solution)/shard_map/ppermute | solution.py:54
  112.6 0.0 collective-permute-start.2
  112.6 0.0 copy-start.1
  112.6 48.0 %collective-permute-done.2 = f32[2,2048,128]{2,1,0:T(8,128)} collective-permute-done((f32[2,2048,128]{2,1,0:T(8,128)}, f32[2,2048,128]{2,1,0:T(8,128)}, u32[]{:S(2)}, u32[]{:S(2)}) %collective-permute-start.2) | collective-permute-done | bytes 2097184 | tf_op jit(solution)/shard_map/ppermute | solution.py:54
  160.6 3.1 %constant_dynamic-update-slice_fusion.7 = f32[2,16384,128]{2,1,0:T(8,128)} fusion(f32[2,2048,128]{2,1,0:T(8,128)} %collective-permute-done.2), kind=kLoop, calls=%fused_computation.32 | loop fusion | bytes 4194304
  163.7 3.0 %constant_dynamic-update-slice_fusion.6 = f32[2,16384,128]{2,1,0:T(8,128)} fusion(f32[2,16384,128]{2,1,0:T(8,128)} %constant_dynamic-update-slice_fusion.7, f32[2,2048,128]{2,1,0:T(8,128)} %collective-permute-done.1), kind=kLoop, calls=%fused_computation.31 | loop fusion | bytes 4194304
  166.7 1.5 constant_dynamic-update-slice_fusion.5
  168.2 3.0 %constant_dynamic-update-slice_fusion.4 = f32[2,16384,128]{2,1,0:T(8,128)} fusion(f32[2,16384,128]{2,1,0:T(8,128)} %constant_dynamic-update-slice_fusion.5, f32[2,1,2,2048,128]{4,3,2,0,1:T(8,128)} %bitcast.42, s32[]{:T(128)S(6)} %select_n.20), kind=kLoop, calls=%fused_computation.29 | loop fusion | bytes 4194308
  171.2 3.1 %constant_dynamic-update-slice_fusion.3 = f32[2,16384,128]{2,1,0:T(8,128)} fusion(f32[2,16384,128]{2,1,0:T(8,128)} %constant_dynamic-update-slice_fusion.4, f32[2,2048,128]{2,1,0:T(8,128)} %collective-permute-done.2), kind=kLoop, calls=%fused_computation.28 | loop fusion | bytes 4194304
  174.3 3.0 %constant_dynamic-update-slice_fusion.2 = f32[2,16384,128]{2,1,0:T(8,128)} fusion(f32[2,16384,128]{2,1,0:T(8,128)} %constant_dynamic-update-slice_fusion.3, f32[2,2048,128]{2,1,0:T(8,128)} %collective-permute-done.1), kind=kLoop, calls=%fused_computation.27 | loop fusion | bytes 4194304
  177.3 1.4 constant_dynamic-update-slice_fusion.1
  178.8 0.0 copy-done.1
  178.8 1.4 constant_dynamic-update-slice_fusion
  180.2 0.0 all-gather.2.cloned.1.call-done
  180.2 0.0 copy-start
  180.2 9.9 %fusion.4 = f32[256,128]{1,0:T(8,128)S(1)} fusion(f32[2,256,8192]{2,1,0:T(8,128)} %all-gather.2.cloned.1.call-done, f32[2,16384,128]{2,1,0:T(8,128)} %constant_dynamic-update-slice_fusion, s32[]{:T(128)S(6)} %select_n.22), kind=kOutput, calls=%fused_computation.4 | convolution fusion | flops 3221225472 | bytes 12713988 | tf_op jit(solution)/shard_map/dot_general | solution.py:17
  190.2 9.8 %fusion.2 = f32[256,128]{1,0:T(8,128)S(1)} fusion(f32[2,256,8192]{2,1,0:T(8,128)} %all-gather.2.cloned.1.call-done, f32[2,16384,128]{2,1,0:T(8,128)} %constant_dynamic-update-slice_fusion, s32[]{:T(128)S(6)} %add.42, s32[]{:T(128)S(6)} %select_n.22), kind=kOutput, calls=%fused_computation.2 | convolution fusion | flops 3221225472 | bytes 12713992 | tf_op jit(solution)/shard_map/dot_general | solution.py:20
  200.0 0.0 copy-done
  200.0 9.6 %fusion.29 = f32[1,256,128]{2,1,0:T(8,128)S(1)} fusion(f32[256,128]{1,0:T(8,128)S(1)} %fusion.2, f32[256,128]{1,0:T(8,128)S(1)} %fusion.4, f32[2,16384,128]{2,1,0:T(8,128)} %constant_dynamic-update-slice_fusion, s32[]{:T(128)S(6)} %select_n.22, s32[]{:T(128)S(6)} %add.42, f32[2,256,8192]{2,1,0:T(8,128)S(1)} %copy-done), kind=kOutput, calls=%fused_computation.22 | convolution fusion | flops 3224436736 | bytes 25559048 | tf_op jit(solution)/shard_map/dot_general | solution.py:23
  209.6 0.7 pad_maximum_fusion
  210.3 0.0 all-reduce.2.cloned.1.call-update
  210.4 21.2 %all-reduce.2.cloned.1.call-done = f32[2,256,128]{2,1,0:T(8,128)} async-done(((f32[2,256,128]{2,1,0:T(8,128)}), f32[2,256,128]{2,1,0:T(8,128)}) %all-reduce.2.cloned.1.call-update) | async-done | bytes 262160 | tf_op jit(solution)/shard_map/psum | solution.py:61
  231.6 1.7 copy.11
  (1 shorter events, 0.0 us)
Async XLA Ops:
  6.5 173.7 %all-gather.2.cloned.1.call-start = ((), (), s32[]{:S(2)}) async-start(), calls=%async_computation | async-start | bytes 20971520 | tf_op jit(solution)/shard_map/all_gather | solution.py:59
  11.3 220.2 %all-reduce.2.cloned.1.call-start = ((), (), s32[]{:S(2)}) async-start(), calls=%async_computation.1 | async-start | bytes 524288 | tf_op jit(solution)/shard_map/psum | solution.py:61
  13.1 50.8 %collective-permute-start = (f32[2,2048,128]{2,1,0:T(8,128)S(1)}, f32[2,2048,128]{2,1,0:T(8,128)S(1)}, u32[]{:S(2)}, u32[]{:S(2)}) collective-permute-start(f32[2,2048,128]{2,1,0:T(8,128)S(1)} %dynamic-slice_bitcast_fusion), channel_id=1, source_target_pairs={{0,4},{4,8},{8,12},{12,0},{1,5},{5,9},{9,13},{13,1},{2,6},{6,10},{... | collective-permute-start | bytes 6291464 | tf_op jit(solution)/shard_map/ppermute | solution.py:54
  63.9 48.7 %collective-permute-start.1 = (f32[2,2048,128]{2,1,0:T(8,128)S(1)}, f32[2,2048,128]{2,1,0:T(8,128)}, u32[]{:S(2)}, u32[]{:S(2)}) collective-permute-start(f32[2,2048,128]{2,1,0:T(8,128)S(1)} %collective-permute-done), channel_id=1, source_target_pairs={{0,4},{4,8},{8,12},{12,0},{1,5},{5,9},{9,13},{13,1},{2,6},{6,10},{... | collective-permute-start | bytes 6291464 | tf_op jit(solution)/shard_map/ppermute | solution.py:54
  112.6 48.1 %collective-permute-start.2 = (f32[2,2048,128]{2,1,0:T(8,128)}, f32[2,2048,128]{2,1,0:T(8,128)}, u32[]{:S(2)}, u32[]{:S(2)}) collective-permute-start(f32[2,2048,128]{2,1,0:T(8,128)} %collective-permute-done.1), channel_id=1, source_target_pairs={{0,4},{4,8},{8,12},{12,0},{1,5},{5,9},{9,13},{13,1},{2,6},{6,10},{... | collective-permute-start | bytes 6291464 | tf_op jit(solution)/shard_map/ppermute | solution.py:54
  112.6 66.2 %copy-start.1 = (f32[2,4096,128]{2,1,0:T(8,128)S(1)}, f32[2,4096,128]{2,1,0:T(8,128)}, u32[]{:S(2)}) copy-start(f32[2,4096,128]{2,1,0:T(8,128)} %param.3) | copy-start | bytes 12582916
  180.2 19.8 %copy-start = (f32[2,256,8192]{2,1,0:T(8,128)S(1)}, f32[2,256,8192]{2,1,0:T(8,128)}, u32[]{:S(2)}) copy-start(f32[2,256,8192]{2,1,0:T(8,128)} %all-gather.2.cloned.1.call-done) | copy-start | bytes 50331652
Sparse Core Ops, SparseCore 0:
  11.4 108.6 all-gather.1
  210.5 21.0 all-reduce.1

commit v2 on v0

--- a/solution.py
+++ b/solution.py
@@ -53,7 +53,7 @@
     accumulate, initial = gauss_fold(right_whole, local_rows, local_cols)
     totals = accumulate(initial, lax.all_gather(left_own, "col", axis=2, tiled=True), jnp.int32(0))
     partial_product = combine_terms(totals)
-    product = lax.psum(partial_product, "layer")
+    product = jnp.sum(lax.all_gather(partial_product, "layer"), axis=0)
     return product
 
 

time: 329 us -> 314 us (0.954)
  waiting for transfers between devices: 277 us -> 253 us
  blocking collectives: 0 us -> 9.12 us
    psum x1 -> x0, waiting for transfers between devices: 23.4 us -> none  [local(): product = lax.psum(partial_product, 'layer')]
    all_gather x0 -> x1, blocking collectives: none -> 9.12 us  [local(): product = jnp.sum(lax.all_gather(partial_product, 'layer'), axis=0)]
  transfers between devices with their start and end apart: 3 -> 2, of which waited for: 3 -> 2; matrix products, arithmetic and copies ran while one was open for 1% -> 1% of each run, Pallas kernels for 0% -> 0%
where the time goes in v2:
time: 314 us
  waiting for transfers between devices  253 us (81%)
  matrix products  28.9 us (9%)
  between operations  13.5 us (4%)
  blocking collectives  9.12 us (3%)
  local copies, waits for them, and re-layouts  7.7 us (2%)
    all_gather x1, waiting for transfers between devices, local(): right_whole = lax.all_gather(right_own, 'row', axis=1, tiled=True)  148 us
    all_gather x1, waiting for transfers between devices, local(): lax.all_gather(left_own, 'col', axis=2, tiled=True)  106 us
    dot_general x1, matrix products, accumulate(): jnp.dot(left_real, right_real, precision=highest, preferred_element_type=...  9.93 us
    dot_general x1, matrix products, accumulate(): jnp.dot(left_imag, right_imag, precision=highest, preferred_element_type=...  9.8 us
    dot_general x1, matrix products, accumulate(): jnp.dot(left_real + left_imag, right_total, precision=highest, preferred_...  9.2 us
    all_gather x1, blocking collectives, local(): product = jnp.sum(lax.all_gather(partial_product, 'layer'), axis=0)  9.12 us
  transfers between devices with their start and end apart: 2, of which 2 were waited for; matrix products, arithmetic and copies ran while one was open for 1% of the time, Pallas kernels for 0%

profile of v2, /device:TPU:0, one launch (start us, length us, event | category | flops | bytes accessed | tf_op | source)
XLA Modules:
  0.0 313.5 jit_solution(16335709139186477865)
XLA Ops:
  6.5 0.0 all-gather.7.cloned.1.call-start
  6.5 3.1 constant_dynamic-slice_fusion
  9.6 0.0 all-gather.7.cloned.1.call-update
  9.6 0.0 all-gather.5.cloned.1.call-start
  9.7 4.6 %constant_dynamic-slice_fusion.1 = f32[2,256,2048]{2,1,0:T(8,128)} fusion(f32[2,256,4096]{2,1,0:T(8,128)} %param.2, s32[]{:T(128)S(6)} %select_n.6), kind=kLoop, calls=%fused_computation.25 | loop fusion | bytes 8388612 | tf_op jit(solution)/shard_map/dynamic_slice | solution.py:48
  14.3 0.0 all-gather.5.cloned.1.call-update
  14.3 147.8 %all-gather.7.cloned.1.call-done = f32[2,1,1,8192,128]{4,3,2,0,1:T(8,128)} async-done(((f32[2,1,1,2048,128]{4,3,2,0,1:T(8,128)}), f32[2,1,1,8192,128]{4,3,2,0,1:T(8,128)}) %all-gather.7.cloned.1.call-update) | async-done | bytes 8388624 | tf_op jit(solution)/shard_map/all_gather | solution.py:52
  162.1 105.7 %all-gather.5.cloned.1.call-done = f32[2,256,8192]{2,1,0:T(8,128)} async-done(((f32[2,256,2048]{2,1,0:T(8,128)}), f32[2,256,8192]{2,1,0:T(8,128)}) %all-gather.5.cloned.1.call-update) | async-done | bytes 16777232 | tf_op jit(solution)/shard_map/all_gather | solution.py:54
  267.8 0.0 copy-start
  267.8 9.9 %fusion.4 = f32[256,128]{1,0:T(8,128)S(1)} fusion(f32[2,256,8192]{2,1,0:T(8,128)} %all-gather.5.cloned.1.call-done, f32[2,1,1,8192,128]{4,3,2,0,1:T(8,128)} %all-gather.7.cloned.1.call-done), kind=kOutput, calls=%fused_computation.4 | convolution fusion | flops 3221225472 | bytes 12713984 | tf_op jit(solution)/shard_map/dot_general | solution.py:17
  277.7 9.8 %fusion.2 = f32[256,128]{1,0:T(8,128)S(1)} fusion(f32[2,256,8192]{2,1,0:T(8,128)} %all-gather.5.cloned.1.call-done, f32[2,1,1,8192,128]{4,3,2,0,1:T(8,128)} %all-gather.7.cloned.1.call-done), kind=kOutput, calls=%fused_computation.2 | convolution fusion | flops 3221225472 | bytes 12713984 | tf_op jit(solution)/shard_map/dot_general | solution.py:20
  287.6 0.0 copy-done
  287.6 9.2 %fusion.29 = f32[1,256,128]{2,1,0:T(8,128)S(1)} fusion(f32[256,128]{1,0:T(8,128)S(1)} %fusion.2, f32[256,128]{1,0:T(8,128)S(1)} %fusion.4, f32[2,1,1,8192,128]{4,3,2,0,1:T(8,128)} %all-gather.7.cloned.1.call-done, f32[2,256,8192]{2,1,0:T(8,128)S(1)} %copy-done), kind=kOutput, calls=%fused_computation.21 | convolution fusion | flops 3224436736 | bytes 25559040 | tf_op jit(solution)/shard_map/dot_general | solution.py:23
  296.8 9.1 %all-gather.1 = f32[4,256,128]{2,1,0:T(8,128)S(1)} all-gather(f32[2,256,128]{2,1,0:T(8,128)S(1)} %pad_maximum_fusion), channel_id=3, replica_groups=mesh['layer'=2,'row'=4,'col'=4] {'layer'}, dimensions={0}, use_global_device_ids=true | all-gather | bytes 786432 | tf_op jit(solution)/shard_map/all_gather | solution.py:56
  305.9 0.7 reduce_sum.9
  (2 shorter events, 0.0 us)
Async XLA Ops:
  6.5 155.6 %all-gather.7.cloned.1.call-start = ((), (), s32[]{:S(2)}) async-start(), calls=%async_computation.1 | async-start | bytes 10485760 | tf_op jit(solution)/shard_map/all_gather | solution.py:52
  9.6 258.2 %all-gather.5.cloned.1.call-start = ((), (), s32[]{:S(2)}) async-start(), calls=%async_computation | async-start | bytes 20971520 | tf_op jit(solution)/shard_map/all_gather | solution.py:54
  267.8 19.8 %copy-start = (f32[2,256,8192]{2,1,0:T(8,128)S(1)}, f32[2,256,8192]{2,1,0:T(8,128)}, u32[]{:S(2)}) copy-start(f32[2,256,8192]{2,1,0:T(8,128)} %all-gather.5.cloned.1.call-done) | copy-start | bytes 50331652
Sparse Core Ops, SparseCore 0:
  9.7 152.3 all-gather.6
  163.7 104.0 all-gather.4
